TPU v7x, 32 devices: a whole 2x2x4 slice. The times are simulated.
32 devices in a mesh: dp: 4 (over y, core), seq: 8 (over z, x).
Axes of the slice: x: 2, y: 2, z: 4, core: 2. Of those that a mesh axis runs over, the one named last changes fastest.
Arguments:
- queries: bfloat16 [32, 2048, 512], P('dp', 'seq'), may hold values from -6 to 6
- enc_keys: bfloat16 [32, 2048, 512], P('dp', 'seq'), may hold values from -6 to 6
- enc_values: bfloat16 [32, 2048, 512], P('dp', 'seq'), may hold values from -6 to 6
- dec_ids: int32 [32, 2048], P('dp', 'seq'), may hold values from 0 to 15, never falling along the last dimension, each value on 1 to 512 neighbouring positions
- enc_ids: int32 [32, 2048], P('dp', 'seq'), may hold values from 0 to 15, never falling along the last dimension, each value on 1 to 512 neighbouring positions
Outputs:
- context: bfloat16 [32, 2048, 512], P('dp', 'seq')
Inputs may be any that keep to these rules, and one draw needn't show every extreme that they name: `dec_ids`: along each row the numbers never fall; every number from 0 to 15 occurs in every row; a document holds 1 to 512 positions of a row, and some document holds exactly 512. `enc_ids`: along each row the numbers never fall; every number from 0 to 15 occurs in every row; a document holds 1 to 512 positions of a row, and some document holds exactly 512.
All inputs are finite; a program needn't handle non-finite values.
Results may differ from a plain program's by a relative error of at most 0.0047.
Values may be sent and summed in bfloat16 or wider, within the bound.
No kernel may reach another device: no remote copies, remote signals or barrier semaphores. Data moves between devices by JAX's collectives and lax.ppermute only.
A program may use at most 128 MiB of HBM per device.

v0:
```python
import jax
import jax.numpy as jnp
from jax import lax
from jax.sharding import PartitionSpec as P

HEAD_DIM = 64
masked_score = -1e30


def shortened(value):

    def short(part):
        return part.astype(jnp.bfloat16) if part.dtype == jnp.float32 else part

    return jax.tree.map(short, value)


def attend_dense(query_row, key_row, value_row, dec_row, enc_row, head_count):
    length = query_row.shape[0]
    query_heads = query_row.reshape(length, head_count, HEAD_DIM)
    key_heads = key_row.reshape(length, head_count, HEAD_DIM)
    value_heads = value_row.reshape(length, head_count, HEAD_DIM)
    query_span = min(512, length)
    pieces = []
    for offset in range(0, length, query_span):
        scores = jnp.einsum(
            "qhd,khd->hqk",
            query_heads[offset : offset + query_span],
            key_heads,
            preferred_element_type=jnp.float32,
        )
        allowed = (dec_row[offset : offset + query_span][:, None] == enc_row[None, :])[None]
        scores = jnp.where(allowed, scores, masked_score)
        row_peak = jnp.max(scores, axis=2, keepdims=True)
        expos = jnp.where(allowed, jnp.exp(scores - row_peak), 0.0)
        row_total = jnp.sum(expos, axis=2, keepdims=True)
        weights = (expos / row_total).astype(jnp.bfloat16)
        summed = jnp.einsum(
            "hqk,khd->qhd", weights, value_heads, preferred_element_type=jnp.float32
        )
        pieces.append(summed.reshape(query_span, head_count * HEAD_DIM).astype(jnp.bfloat16))
    return jnp.concatenate(pieces, axis=0)


def local(queries, enc_keys, enc_values, dec_ids, enc_ids):
    group = lax.axis_size("seq")
    dec_spread = jnp.broadcast_to(
        dec_ids.astype(jnp.bfloat16)[:, :, None], (dec_ids.shape[0], dec_ids.shape[1], group)
    )
    enc_spread = jnp.broadcast_to(
        enc_ids.astype(jnp.bfloat16)[:, :, None], (enc_ids.shape[0], enc_ids.shape[1], group)
    )
    members = (
        lax.all_to_all(queries, "seq", split_axis=2, concat_axis=1, tiled=True),
        lax.all_to_all(enc_keys, "seq", split_axis=2, concat_axis=1, tiled=True),
        lax.all_to_all(enc_values, "seq", split_axis=2, concat_axis=1, tiled=True),
        lax.all_to_all(dec_spread, "seq", split_axis=2, concat_axis=1, tiled=True),
        lax.all_to_all(enc_spread, "seq", split_axis=2, concat_axis=1, tiled=True),
    )
    dec_rows = members[3][:, :, 0].astype(jnp.int32)
    enc_rows = members[4][:, :, 0].astype(jnp.int32)
    query_rows = members[0]
    key_rows = members[1]
    value_rows = members[2]
    head_count = query_rows.shape[2] // HEAD_DIM

    def one_row(members):
        return attend_dense(members[0], members[1], members[2], members[3], members[4], head_count)

    attended = lax.map(one_row, (query_rows, key_rows, value_rows, dec_rows, enc_rows))
    return lax.all_to_all(
        shortened(attended), "seq", split_axis=1, concat_axis=2, tiled=True
    ).astype(attended.dtype)


def solution(mesh):
    in_specs = (
        P("dp", "seq", None),
        P("dp", "seq", None),
        P("dp", "seq", None),
        P("dp", "seq"),
        P("dp", "seq"),
    )
    out_specs = P("dp", "seq", None)
    return jax.shard_map(local, mesh=mesh, in_specs=in_specs, out_specs=out_specs, check_vma=False)
```

profile of v0, /device:TPU:0, one launch (start us, length us, event | category | flops | bytes accessed | tf_op | source)
XLA Modules:
  0.0 412.9 jit_solution(16733577638339409978)
XLA Ops:
  1.3 7.3 %all-to-all-start.1 = ((bf16[8,256,8]{1,0,2:T(8,128)(2,1)}), bf16[8,256,8]{1,0,2:T(8,128)(2,1)S(1)}, u32[]{:S(2)}, u32[]{:S(2)}) async-start(bf16[8,256,8]{1,0,2:T(8,128)(2,1)} %broadcast_in_dim.23), calls=%async_computation.1 | async-start | bytes 65536 | tf_op jit(solution)/shard_map/all_to_all | solution.py:57
  9.3 6.0 %all-to-all-done.1 = bf16[8,256,8]{1,0,2:T(8,128)(2,1)S(1)} async-done(((bf16[8,256,8]{1,0,2:T(8,128)(2,1)}), bf16[8,256,8]{1,0,2:T(8,128)(2,1)S(1)}, u32[]{:S(2)}, u32[]{:S(2)}) %all-to-all-start.1) | async-done | bytes 32800 | tf_op jit(solution)/shard_map/all_to_all | solution.py:57
  19.2 4.5 %copy.25 = bf16[8,256,512]{1,0,2:T(8,128)(2,1)} copy(bf16[8,256,512]{2,1,0:T(8,128)(2,1)} %param.9) | data formatting | bytes 4194304 | tf_op args[2]
  29.7 4.5 %copy.28 = bf16[8,256,512]{1,0,2:T(8,128)(2,1)} copy(bf16[8,256,512]{2,1,0:T(8,128)(2,1)} %param.7) | data formatting | bytes 4194304 | tf_op args[0]
  34.2 42.1 %all-to-all-done = bf16[8,256,512]{1,0,2:T(8,128)(2,1)S(1)} async-done(((bf16[8,256,512]{1,0,2:T(8,128)(2,1)}), bf16[8,256,512]{1,0,2:T(8,128)(2,1)S(1)}, u32[]{:S(2)}, u32[]{:S(2)}) %all-to-all-start) | async-done | bytes 2097184 | tf_op jit(solution)/shard_map/all_to_all | solution.py:56
  76.3 4.4 %all-to-all-start.3 = ((bf16[8,256,512]{1,0,2:T(8,128)(2,1)}), bf16[8,256,512]{1,0,2:T(8,128)(2,1)}, u32[]{:S(2)}, u32[]{:S(2)}) async-start(bf16[8,256,512]{1,0,2:T(8,128)(2,1)} %copy.28), calls=%async_computation.3 | async-start | bytes 4194304 | tf_op jit(solution)/shard_map/all_to_all | solution.py:54
  80.7 4.5 %copy.31 = bf16[8,256,512]{1,0,2:T(8,128)(2,1)} copy(bf16[8,256,512]{2,1,0:T(8,128)(2,1)} %param.8) | data formatting | bytes 4194304 | tf_op args[1]
  85.2 43.1 %all-to-all-done.3 = bf16[8,256,512]{1,0,2:T(8,128)(2,1)} async-done(((bf16[8,256,512]{1,0,2:T(8,128)(2,1)}), bf16[8,256,512]{1,0,2:T(8,128)(2,1)}, u32[]{:S(2)}, u32[]{:S(2)}) %all-to-all-start.3) | async-done | bytes 2097184 | tf_op jit(solution)/shard_map/all_to_all | solution.py:54
  128.3 4.4 %all-to-all-start.4 = ((bf16[8,256,512]{1,0,2:T(8,128)(2,1)}), bf16[8,256,512]{1,0,2:T(8,128)(2,1)}, u32[]{:S(2)}, u32[]{:S(2)}) async-start(bf16[8,256,512]{1,0,2:T(8,128)(2,1)} %copy.31), calls=%async_computation.4 | async-start | bytes 4194304 | tf_op jit(solution)/shard_map/all_to_all | solution.py:55
  136.3 5.0 %copy.44 = bf16[8,8,256,64]{3,2,1,0:T(8,128)(2,1)} copy(bf16[8,8,256,64]{2,0,3,1:T(8,128)(2,1)} %bitcast.36) | data formatting | bytes 4194304 | tf_op jit(solution)/shard_map/while | solution.py:70
  141.3 39.2 %all-to-all-done.4 = bf16[8,256,512]{1,0,2:T(8,128)(2,1)} async-done(((bf16[8,256,512]{1,0,2:T(8,128)(2,1)}), bf16[8,256,512]{1,0,2:T(8,128)(2,1)}, u32[]{:S(2)}, u32[]{:S(2)}) %all-to-all-start.4) | async-done | bytes 2097184 | tf_op jit(solution)/shard_map/all_to_all | solution.py:55
  180.5 5.0 %copy.46 = bf16[8,8,256,64]{3,2,1,0:T(8,128)(2,1)} copy(bf16[8,8,256,64]{2,0,3,1:T(8,128)(2,1)} %bitcast.40) | data formatting | bytes 4194304 | tf_op jit(solution)/shard_map/while | solution.py:70
  185.5 150.7 %while.10 = (s32[]{:T(128)}, bf16[8,2048,64]{1,2,0:T(8,128)(2,1)S(1)}, bf16[8,2048,64]{2,1,0:T(8,128)(2,1)}, s32[8,2048]{1,0:T(8,128)S(1)}, s32[8,2048]{1,0:T(8,...) while((s32[]{:T(128)}, ...), condition=%wide.region_9.10_spmd, body=%wide.region_0.9_spmd.sunk | while | flops 1133637632 | bytes 72773864 | solution.py:70
  191.2 3.9 fusion.85
  210.1 3.9 fusion.85
  228.9 3.9 fusion.85
  247.7 3.9 fusion.85
  266.6 3.9 fusion.85
  323.1 3.9 fusion.85
  336.2 4.3 %copy.37 = bf16[8,2048,64]{2,0,1:T(8,128)(2,1)} copy(bf16[8,2048,64]{1,2,0:T(8,128)(2,1)S(1)} %get-tuple-element.42) | data formatting | bytes 4194304 | tf_op jit(solution)/shard_map/while | solution.py:70
  340.5 6.4 %reshape.166 = bf16[8,2,65536]{2,1,0:T(2,128)(2,1)S(1)} reshape(bf16[2048,8,64]{2,1,0:T(8,128)(2,1)} %bitcast.147) | data formatting | bytes 4194304
  346.8 51.8 %all_to_all.90 = bf16[8,2,65536]{2,1,0:T(2,128)(2,1)} all-to-all(bf16[8,2,65536]{2,1,0:T(2,128)(2,1)S(1)} %reshape.166), channel_id=1, replica_groups=mesh['dp'=4,'seq'=8] {'seq'}, dimensions={0} | all-to-all | bytes 4194304 | tf_op jit(solution)/shard_map/all_to_all | solution.py:71
  398.7 7.4 %reshape.167 = bf16[2048,8,64]{2,1,0:T(8,128)(2,1)} reshape(bf16[8,2,65536]{2,1,0:T(2,128)(2,1)} %all_to_all.90) | data formatting | bytes 4194304
  406.1 4.5 %copy.39 = bf16[8,256,8,64]{1,3,2,0:T(8,128)(2,1)S(1)} copy(bf16[8,256,8,64]{3,0,1,2:T(8,128)(2,1)} %bitcast.148) | data formatting | bytes 4194304 | tf_op jit(solution)/shard_map/all_to_all | solution.py:71
  (120 shorter events, 144.7 us)
Async XLA Ops:
  1.3 14.0 %all-to-all-start.1 = ((bf16[8,256,8]{1,0,2:T(8,128)(2,1)}), bf16[8,256,8]{1,0,2:T(8,128)(2,1)S(1)}, u32[]{:S(2)}, u32[]{:S(2)}) async-start(bf16[8,256,8]{1,0,2:T(8,128)(2,1)} %broadcast_in_dim.23), calls=%async_computation.1 | async-start | bytes 65536 | tf_op jit(solution)/shard_map/all_to_all | solution.py:57
  15.9 10.0 %all-to-all-start.2 = ((bf16[8,256,8]{1,0,2:T(8,128)(2,1)}), bf16[8,256,8]{1,0,2:T(8,128)(2,1)S(1)}, u32[]{:S(2)}, u32[]{:S(2)}) async-start(bf16[8,256,8]{1,0,2:T(8,128)(2,1)} %broadcast_in_dim.24), calls=%async_computation.2 | async-start | bytes 65536 | tf_op jit(solution)/shard_map/all_to_all | solution.py:58
  25.9 50.4 %all-to-all-start = ((bf16[8,256,512]{1,0,2:T(8,128)(2,1)}), bf16[8,256,512]{1,0,2:T(8,128)(2,1)S(1)}, u32[]{:S(2)}, u32[]{:S(2)}) async-start(bf16[8,256,512]{1,0,2:T(8,128)(2,1)} %copy.25), calls=%async_computation | async-start | bytes 4194304 | tf_op jit(solution)/shard_map/all_to_all | solution.py:56
  76.3 52.0 %all-to-all-start.3 = ((bf16[8,256,512]{1,0,2:T(8,128)(2,1)}), bf16[8,256,512]{1,0,2:T(8,128)(2,1)}, u32[]{:S(2)}, u32[]{:S(2)}) async-start(bf16[8,256,512]{1,0,2:T(8,128)(2,1)} %copy.28), calls=%async_computation.3 | async-start | bytes 4194304 | tf_op jit(solution)/shard_map/all_to_all | solution.py:54
  128.3 52.2 %all-to-all-start.4 = ((bf16[8,256,512]{1,0,2:T(8,128)(2,1)}), bf16[8,256,512]{1,0,2:T(8,128)(2,1)}, u32[]{:S(2)}, u32[]{:S(2)}) async-start(bf16[8,256,512]{1,0,2:T(8,128)(2,1)} %copy.31), calls=%async_computation.4 | async-start | bytes 4194304 | tf_op jit(solution)/shard_map/all_to_all | solution.py:55
  141.3 44.2 %copy-start.1 = (bf16[8,2048,64]{1,2,0:T(8,128)(2,1)S(1)}, bf16[8,2048,64]{1,2,0:T(8,128)(2,1)}, u32[]{:S(2)}) copy-start(bf16[8,2048,64]{1,2,0:T(8,128)(2,1)} %custom-call) | copy-start | bytes 6291460
  191.2 3.9 copy-start
  210.0 3.9 copy-start
  228.9 3.9 copy-start
  247.7 3.9 copy-start
  266.6 3.9 copy-start
  285.4 3.9 copy-start
  304.2 3.9 copy-start
  323.1 3.9 copy-start
where the time goes:
time: 415 us; the launch traced here: 413 us
  waiting for transfers between devices  133 us (32%)
  matrix products  122 us (29%)
  local copies, waits for them, and re-layouts  54 us (13%)
  blocking collectives  51.8 us (12%)
  other arithmetic  29 us (7%)
  starting transfers between devices  23.1 us (6%)
    dot_general x32, matrix products, attend_dense(): jnp.einsum('qhd,khd->hqk', query_heads[offset:offset + query_span], key_h...  75.9 us
    all_to_all x1, blocking collectives, local(): lax.all_to_all(shortened(attended), 'seq', split_axis=1, concat_axis=2, t...  51.8 us
    dot_general x32, matrix products, attend_dense(): jnp.einsum('hqk,khd->qhd', weights, value_heads, preferred_element_type=j...  45.9 us
    all_to_all x1, waiting for transfers between devices, local(): lax.all_to_all(queries, 'seq', split_axis=2, concat_axis=1, tiled=True)  43.1 us
    all_to_all x1, waiting for transfers between devices, local(): lax.all_to_all(enc_values, 'seq', split_axis=2, concat_axis=1, tiled=True)  42.1 us
    all_to_all x1, waiting for transfers between devices, local(): lax.all_to_all(enc_keys, 'seq', split_axis=2, concat_axis=1, tiled=True)  39.2 us
    reduce_sum x8, other arithmetic, attend_dense(): row_total = jnp.sum(expos, axis=2, keepdims=True)  27.4 us
    unnamed x7, local copies, waits for them, and re-layouts  27.3 us
  transfers between devices with their start and end apart: 5, of which 5 were waited for; matrix products, arithmetic and copies ran while one was open for 6% of the time, Pallas kernels for 0%

commit v1 on v0

--- a/solution.py
+++ b/solution.py
@@ -1,3 +1,4 @@
+import functools
 import jax
 import jax.numpy as jnp
 from jax import lax
@@ -5,6 +6,29 @@
 
 HEAD_DIM = 64
 masked_score = -1e30
+
+
+def search_spots(row_data, chip_axis, dim_i, dim_at):
+    local_now, found_now = (lax.axis_size(chip_axis), lax.axis_index(chip_axis))
+    after = row_data.shape[dim_i] // local_now
+    work_now = jnp.roll(row_data, -found_now * after, axis=dim_i)
+    row_list = [lax.slice_in_dim(work_now, 0, after, axis=dim_i)]
+    j = 1
+    while j < local_now:
+        main = lax.slice_in_dim(work_now, j * after, (j + 1) * after, axis=dim_i)
+        row_list.append(
+            lax.ppermute(
+                main,
+                axis_name=chip_axis,
+                perm=[(i0, (i0 + j) % local_now) for i0 in range(local_now)],
+            )
+        )
+        j = j + 1
+    mixed_arr = jnp.concatenate(row_list[::-1], axis=dim_at)
+    return jnp.roll(mixed_arr, (found_now + 1) * row_list[0].shape[dim_at], axis=dim_at)
+
+
+number_space = functools.partial(search_spots, chip_axis="seq", dim_i=2, dim_at=1)
 
 
 def shortened(value):
@@ -53,7 +77,7 @@
     members = (
         lax.all_to_all(queries, "seq", split_axis=2, concat_axis=1, tiled=True),
         lax.all_to_all(enc_keys, "seq", split_axis=2, concat_axis=1, tiled=True),
-        lax.all_to_all(enc_values, "seq", split_axis=2, concat_axis=1, tiled=True),
+        number_space(enc_values),
         lax.all_to_all(dec_spread, "seq", split_axis=2, concat_axis=1, tiled=True),
         lax.all_to_all(enc_spread, "seq", split_axis=2, concat_axis=1, tiled=True),
     )

time: 415 us -> 464 us (1.12)
  starting transfers between devices: 23.1 us -> 76.9 us
  waiting for transfers between devices: 133 us -> 123 us
    ppermute x0 -> x7, waiting for transfers between devices: none -> 72.3 us  [search_spots(): lax.ppermute(main, axis_name=chip_axis, perm=[(i0, (i0 + j) % local_now)...]
    ppermute x0 -> x7, starting transfers between devices: none -> 58.1 us  [search_spots(): lax.ppermute(main, axis_name=chip_axis, perm=[(i0, (i0 + j) % local_now)...]
    all_to_all x1 -> x0, waiting for transfers between devices: 42.1 us -> none  [local(): lax.all_to_all(enc_values, 'seq', split_axis=2, concat_axis=1, tiled=True)]
    all_to_all x1, waiting for transfers between devices: 39.2 us -> 0.01 us  [local(): lax.all_to_all(enc_keys, 'seq', split_axis=2, concat_axis=1, tiled=True)]
    while x4 -> x3, local copies, waits for them, and re-layouts: 17.8 us -> 12.9 us  [local(): lax.map(one_row, (query_rows, key_rows, value_rows, dec_rows, enc_rows))]
    unnamed x7 -> x25, local copies, waits for them, and re-layouts: 27.3 us -> 30.2 us
  transfers between devices with their start and end apart: 5 -> 11, of which waited for: 5 -> 6; matrix products, arithmetic and copies ran while one was open for 6% -> 6% of each run, Pallas kernels for 0% -> 0%
where the time goes in v1:
time: 464 us; the launch traced here: 462 us
  waiting for transfers between devices  123 us (27%)
  matrix products  122 us (26%)
  starting transfers between devices  76.9 us (17%)
  local copies, waits for them, and re-layouts  56.8 us (12%)
  blocking collectives  50.8 us (11%)
  other arithmetic  32.4 us (7%)
    dot_general x32, matrix products, attend_dense(): jnp.einsum('qhd,khd->hqk', query_heads[offset:offset + query_span], key_h...  75.8 us
    ppermute x7, waiting for transfers between devices, search_spots(): lax.ppermute(main, axis_name=chip_axis, perm=[(i0, (i0 + j) % local_now)...  72.3 us
    ppermute x7, starting transfers between devices, search_spots(): lax.ppermute(main, axis_name=chip_axis, perm=[(i0, (i0 + j) % local_now)...  58.1 us
    all_to_all x1, blocking collectives, local(): lax.all_to_all(shortened(attended), 'seq', split_axis=1, concat_axis=2, t...  50.8 us
    dot_general x32, matrix products, attend_dense(): jnp.einsum('hqk,khd->qhd', weights, value_heads, preferred_element_type=j...  45.8 us
    all_to_all x1, waiting for transfers between devices, local(): lax.all_to_all(queries, 'seq', split_axis=2, concat_axis=1, tiled=True)  42.1 us
    unnamed x25, local copies, waits for them, and re-layouts  30.2 us
    reduce_sum x8, other arithmetic, attend_dense(): row_total = jnp.sum(expos, axis=2, keepdims=True)  27.4 us
  transfers between devices with their start and end apart: 11, of which 6 were waited for; matrix products, arithmetic and copies ran while one was open for 6% of the time, Pallas kernels for 0%

profile of v1, /device:TPU:0, one launch (start us, length us, event | category | flops | bytes accessed | tf_op | source)
XLA Modules:
  0.0 461.8 jit_solution(1685660452593663048)
XLA Ops:
  1.3 7.3 %all-to-all-start = ((bf16[8,256,8]{1,0,2:T(8,128)(2,1)}), bf16[8,256,8]{1,0,2:T(8,128)(2,1)S(1)}, u32[]{:S(2)}, u32[]{:S(2)}) async-start(bf16[8,256,8]{1,0,2:T(8,128)(2,1)} %broadcast_in_dim.23), calls=%async_computation | async-start | bytes 65536 | tf_op jit(solution)/shard_map/all_to_all | solution.py:81
  9.3 6.0 %all-to-all-done = bf16[8,256,8]{1,0,2:T(8,128)(2,1)S(1)} async-done(((bf16[8,256,8]{1,0,2:T(8,128)(2,1)}), bf16[8,256,8]{1,0,2:T(8,128)(2,1)S(1)}, u32[]{:S(2)}, u32[]{:S(2)}) %all-to-all-start) | async-done | bytes 32800 | tf_op jit(solution)/shard_map/all_to_all | solution.py:81
  19.2 4.5 copy.20
  29.7 4.5 copy.23
  34.2 42.1 %all-to-all-done.2 = bf16[8,256,512]{1,0,2:T(8,128)(2,1)S(1)} async-done(((bf16[8,256,512]{1,0,2:T(8,128)(2,1)}), bf16[8,256,512]{1,0,2:T(8,128)(2,1)S(1)}, u32[]{:S(2)}, u32[]{:S(2)}) %all-to-all-start.2) | async-done | bytes 2097184 | tf_op jit(solution)/shard_map/all_to_all | solution.py:78
  76.3 4.4 all-to-all-start.3
  86.6 4.8 %collective-permute-start = (bf16[8,256,64]{2,1,0:T(8,128)(2,1)}, bf16[8,256,64]{2,1,0:T(8,128)(2,1)S(1)}, u32[]{:S(2)}, u32[]{:S(2)}) collective-permute-start(bf16[8,256,64]{2,1,0:T(8,128)(2,1)} %get-tuple-element.91), channel_id=1, source_target_pairs={{0,7},{1,0},{2,1},{3,2},{4,3},{5,4},{6,5},{7,6},{8,15},{9,8},{10,9... | collective-permute-start | bytes 786440 | tf_op jit(solution)/shard_map/ppermute | solution.py:20
  94.9 32.6 %collective-permute-done = bf16[8,256,64]{2,1,0:T(8,128)(2,1)S(1)} collective-permute-done((bf16[8,256,64]{2,1,0:T(8,128)(2,1)}, bf16[8,256,64]{2,1,0:T(8,128)(2,1)S(1)}, u32[]{:S(2)}, u32[]{:S(2)}) %collective-permute-start) | collective-permute-done | bytes 262176 | tf_op jit(solution)/shard_map/ppermute | solution.py:20
  127.5 11.2 %collective-permute-done.1 = bf16[8,256,64]{2,1,0:T(8,128)(2,1)S(1)} collective-permute-done((bf16[8,256,64]{2,1,0:T(8,128)(2,1)}, bf16[8,256,64]{2,1,0:T(8,128)(2,1)S(1)}, u32[]{:S(2)}, u32[]{:S(2)}) %collective-permute-start.1) | collective-permute-done | bytes 262176 | tf_op jit(solution)/shard_map/ppermute | solution.py:20
  138.7 49.8 %collective-permute-start.6 = (bf16[8,256,64]{2,1,0:T(8,128)(2,1)}, bf16[8,256,64]{2,1,0:T(8,128)(2,1)S(1)}, u32[]{:S(2)}, u32[]{:S(2)}) collective-permute-start(bf16[8,256,64]{2,1,0:T(8,128)(2,1)} %get-tuple-element.85), channel_id=1, source_target_pairs={{0,1},{1,2},{2,3},{3,4},{4,5},{5,6},{6,7},{7,0},{8,9},{9,10},{10,1... | collective-permute-start | bytes 786440 | tf_op jit(solution)/shard_map/ppermute | solution.py:20
  189.7 28.6 %collective-permute-done.3 = bf16[8,256,64]{2,1,0:T(8,128)(2,1)} collective-permute-done((bf16[8,256,64]{2,1,0:T(8,128)(2,1)}, bf16[8,256,64]{2,1,0:T(8,128)(2,1)}, u32[]{:S(2)}, u32[]{:S(2)}) %collective-permute-start.3) | collective-permute-done | bytes 262176 | tf_op jit(solution)/shard_map/ppermute | solution.py:20
  230.4 5.1 %copy.35 = bf16[8,8,256,64]{3,2,1,0:T(8,128)(2,1)} copy(bf16[8,8,256,64]{2,0,3,1:T(8,128)(2,1)} %bitcast.36) | data formatting | bytes 4194304 | tf_op jit(solution)/shard_map/while | solution.py:94
  235.6 150.6 %while.10 = (s32[]{:T(128)}, bf16[8,2048,64]{1,2,0:T(8,128)(2,1)S(1)}, bf16[8,2048,64]{2,1,0:T(8,128)(2,1)}, s32[8,2048]{1,0:T(8,128)S(1)}, s32[8,2048]{1,0:T(8,...) while((s32[]{:T(128)}, ...), condition=%wide.region_9.10_spmd, body=%wide.region_0.9_spmd.sunk | while | flops 1133637632 | bytes 72773864 | solution.py:94
  241.3 3.9 fusion.87
  260.1 3.9 fusion.87
  279.0 3.9 fusion.87
  297.8 3.9 fusion.87
  316.6 3.9 fusion.87
  373.1 3.9 fusion.87
  386.2 4.3 copy.28
  390.5 6.4 %reshape.166 = bf16[8,2,65536]{2,1,0:T(2,128)(2,1)S(1)} reshape(bf16[2048,8,64]{2,1,0:T(8,128)(2,1)} %bitcast.143) | data formatting | bytes 4194304
  396.9 50.8 %all_to_all.72 = bf16[8,2,65536]{2,1,0:T(2,128)(2,1)} all-to-all(bf16[8,2,65536]{2,1,0:T(2,128)(2,1)S(1)} %reshape.166), channel_id=1, replica_groups=mesh['dp'=4,'seq'=8] {'seq'}, dimensions={0} | all-to-all | bytes 4194304 | tf_op jit(solution)/shard_map/all_to_all | solution.py:95
  447.6 7.4 %reshape.167 = bf16[2048,8,64]{2,1,0:T(8,128)(2,1)} reshape(bf16[8,2,65536]{2,1,0:T(2,128)(2,1)} %all_to_all.72) | data formatting | bytes 4194304
  455.0 4.5 copy.30
  (153 shorter events, 163.8 us)
Async XLA Ops:
  1.3 14.0 %all-to-all-start = ((bf16[8,256,8]{1,0,2:T(8,128)(2,1)}), bf16[8,256,8]{1,0,2:T(8,128)(2,1)S(1)}, u32[]{:S(2)}, u32[]{:S(2)}) async-start(bf16[8,256,8]{1,0,2:T(8,128)(2,1)} %broadcast_in_dim.23), calls=%async_computation | async-start | bytes 65536 | tf_op jit(solution)/shard_map/all_to_all | solution.py:81
  15.9 10.0 %all-to-all-start.1 = ((bf16[8,256,8]{1,0,2:T(8,128)(2,1)}), bf16[8,256,8]{1,0,2:T(8,128)(2,1)S(1)}, u32[]{:S(2)}, u32[]{:S(2)}) async-start(bf16[8,256,8]{1,0,2:T(8,128)(2,1)} %broadcast_in_dim.24), calls=%async_computation.1 | async-start | bytes 65536 | tf_op jit(solution)/shard_map/all_to_all | solution.py:82
  25.8 50.4 %all-to-all-start.2 = ((bf16[8,256,512]{1,0,2:T(8,128)(2,1)}), bf16[8,256,512]{1,0,2:T(8,128)(2,1)S(1)}, u32[]{:S(2)}, u32[]{:S(2)}) async-start(bf16[8,256,512]{1,0,2:T(8,128)(2,1)} %copy.20), calls=%async_computation.2 | async-start | bytes 4194304 | tf_op jit(solution)/shard_map/all_to_all | solution.py:78
  76.3 4.4 copy-start
  76.3 154.1 %all-to-all-start.3 = ((bf16[8,256,512]{1,0,2:T(8,128)(2,1)}), bf16[8,256,512]{1,0,2:T(8,128)(2,1)}, u32[]{:S(2)}, u32[]{:S(2)}) async-start(bf16[8,256,512]{1,0,2:T(8,128)(2,1)} %copy.23), calls=%async_computation.3 | async-start | bytes 4194304 | tf_op jit(solution)/shard_map/all_to_all | solution.py:79
  86.6 40.9 %collective-permute-start = (bf16[8,256,64]{2,1,0:T(8,128)(2,1)}, bf16[8,256,64]{2,1,0:T(8,128)(2,1)S(1)}, u32[]{:S(2)}, u32[]{:S(2)}) collective-permute-start(bf16[8,256,64]{2,1,0:T(8,128)(2,1)} %get-tuple-element.91), channel_id=1, source_target_pairs={{0,7},{1,0},{2,1},{3,2},{4,3},{5,4},{6,5},{7,6},{8,15},{9,8},{10,9... | collective-permute-start | bytes 786440 | tf_op jit(solution)/shard_map/ppermute | solution.py:20
  91.4 47.3 %collective-permute-start.1 = (bf16[8,256,64]{2,1,0:T(8,128)(2,1)}, bf16[8,256,64]{2,1,0:T(8,128)(2,1)S(1)}, u32[]{:S(2)}, u32[]{:S(2)}) collective-permute-start(bf16[8,256,64]{2,1,0:T(8,128)(2,1)} %get-tuple-element.90), channel_id=1, source_target_pairs={{0,6},{1,7},{2,0},{3,1},{4,2},{5,3},{6,4},{7,5},{8,14},{9,15},{10,... | collective-permute-start | bytes 786440 | tf_op jit(solution)/shard_map/ppermute | solution.py:20
  91.9 96.7 %collective-permute-start.2 = (bf16[8,256,64]{2,1,0:T(8,128)(2,1)}, bf16[8,256,64]{2,1,0:T(8,128)(2,1)}, u32[]{:S(2)}, u32[]{:S(2)}) collective-permute-start(bf16[8,256,64]{2,1,0:T(8,128)(2,1)} %get-tuple-element.89), channel_id=1, source_target_pairs={{0,5},{1,6},{2,7},{3,0},{4,1},{5,2},{6,3},{7,4},{8,13},{9,14},{10,... | collective-permute-start | bytes 786440 | tf_op jit(solution)/shard_map/ppermute | solution.py:20
  91.9 126.4 %collective-permute-start.3 = (bf16[8,256,64]{2,1,0:T(8,128)(2,1)}, bf16[8,256,64]{2,1,0:T(8,128)(2,1)}, u32[]{:S(2)}, u32[]{:S(2)}) collective-permute-start(bf16[8,256,64]{2,1,0:T(8,128)(2,1)} %get-tuple-element.88), channel_id=1, source_target_pairs={{0,4},{1,5},{2,6},{3,7},{4,0},{5,1},{6,2},{7,3},{8,12},{9,13},{10,... | collective-permute-start | bytes 786440 | tf_op jit(solution)/shard_map/ppermute | solution.py:20
  94.8 124.6 %collective-permute-start.4 = (bf16[8,256,64]{2,1,0:T(8,128)(2,1)}, bf16[8,256,64]{2,1,0:T(8,128)(2,1)}, u32[]{:S(2)}, u32[]{:S(2)}) collective-permute-start(bf16[8,256,64]{2,1,0:T(8,128)(2,1)} %get-tuple-element.87), channel_id=1, source_target_pairs={{0,3},{1,4},{2,5},{3,6},{4,7},{5,0},{6,1},{7,2},{8,11},{9,12},{10,... | collective-permute-start | bytes 786440 | tf_op jit(solution)/shard_map/ppermute | solution.py:20
  127.4 93.1 %collective-permute-start.5 = (bf16[8,256,64]{2,1,0:T(8,128)(2,1)}, bf16[8,256,64]{2,1,0:T(8,128)(2,1)S(1)}, u32[]{:S(2)}, u32[]{:S(2)}) collective-permute-start(bf16[8,256,64]{2,1,0:T(8,128)(2,1)} %get-tuple-element.86), channel_id=1, source_target_pairs={{0,2},{1,3},{2,4},{3,5},{4,6},{5,7},{6,0},{7,1},{8,10},{9,11},{10,... | collective-permute-start | bytes 786440 | tf_op jit(solution)/shard_map/ppermute | solution.py:20
  138.7 81.9 %collective-permute-start.6 = (bf16[8,256,64]{2,1,0:T(8,128)(2,1)}, bf16[8,256,64]{2,1,0:T(8,128)(2,1)S(1)}, u32[]{:S(2)}, u32[]{:S(2)}) collective-permute-start(bf16[8,256,64]{2,1,0:T(8,128)(2,1)} %get-tuple-element.85), channel_id=1, source_target_pairs={{0,1},{1,2},{2,3},{3,4},{4,5},{5,6},{6,7},{7,0},{8,9},{9,10},{10,1... | collective-permute-start | bytes 786440 | tf_op jit(solution)/shard_map/ppermute | solution.py:20
  224.6 2.3 copy-start.1
  230.4 5.1 %copy-start.3 = (bf16[8,2048,64]{1,2,0:T(8,128)(2,1)S(1)}, bf16[8,2048,64]{1,2,0:T(8,128)(2,1)}, u32[]{:S(2)}) copy-start(bf16[8,2048,64]{1,2,0:T(8,128)(2,1)} %custom-call.1) | copy-start | bytes 6291460
  241.3 3.9 copy-start.2
  260.1 3.9 copy-start.2
  279.0 3.9 copy-start.2
  297.8 3.9 copy-start.2
  316.6 3.9 copy-start.2
  335.4 3.9 copy-start.2
  354.3 3.9 copy-start.2
  373.1 3.9 copy-start.2
